TPU v7x, 32 devices: a whole 2x2x4 slice. The times are simulated.
32 devices in a mesh: up: 8 (over z, core), down: 4 (over y, x).
Axes of the slice: x: 2, y: 2, z: 4, core: 2. Of those that a mesh axis runs over, the one named last changes fastest.
Arguments:
- deltas: bfloat16 [256, 4096], P('down', 'up'), may hold values from -6 to 6
- gradients: bfloat16 [256, 4096], P('up', 'down'), may hold values from -0.375 to 0.375
- up_blocks: int32 [8, 16], P(None, 'up'), may hold values from 0 to 3, as said below
- down_blocks: int32 [16], P('down'), may hold values from 0 to 7, as said below
- decoder: bfloat16 [4096, 4608], P('up', 'down'), may hold values from -0.09375 to 0.09375
- encoder: bfloat16 [4608, 4096], P('up', 'down'), may hold values from -6 to 6
Outputs:
- edge_scores: float32 [4096, 4096], P('up', 'down')
Inputs may be any that keep to these rules, and one draw needn't show every extreme that they name: `up_blocks`: for each window and each index i of up, the 2 entries in columns i * 2 to (i + 1) * 2 - 1 are distinct. `down_blocks`: for each index j of down, the 4 entries j * 4 to (j + 1) * 4 - 1 are distinct.
All inputs are finite; a program needn't handle non-finite values.
Results may differ from a plain program's by a relative error of at most 0.0003.
Values may be sent and summed in bfloat16 or wider, within the bound.
A program may use at most 64 MiB of HBM per device.

v0:
```python
import jax
import jax.numpy as jnp
from jax import lax
from jax.sharding import PartitionSpec as P

UF_DEV = 512
VF_DEV = 1024
BLOCK = 128
DACT = 4
WIN = 32


def local(deltas, gradients, up_blocks, down_blocks, decoder, encoder):
    token_deltas = lax.all_gather(deltas, "down", axis=0, tiled=True)
    token_grads = lax.all_gather(gradients, "up", axis=0, tiled=True)
    tokens_all = token_deltas.shape[0]
    windows = tokens_all // WIN
    row_blocks = UF_DEV // BLOCK
    col_blocks = VF_DEV // BLOCK
    local_ids = jnp.arange(row_blocks, dtype=jnp.int32)
    block_on = jnp.any(up_blocks[:, :, None] == local_ids[None, None, :], axis=1)
    masked = token_deltas.reshape(windows, WIN, row_blocks, BLOCK) * block_on[
        :, None, :, None
    ].astype(token_deltas.dtype)
    masked = masked.reshape(tokens_all, UF_DEV)
    dec_whole = lax.all_gather(decoder, "down", axis=1, tiled=True)
    enc_height = encoder.shape[0]
    enc_used = jnp.take(
        encoder.reshape(enc_height, col_blocks, BLOCK), down_blocks, axis=1
    ).reshape(enc_height, DACT * BLOCK)
    virtual = jnp.dot(
        dec_whole,
        lax.all_gather(enc_used, "up", axis=0, tiled=True),
        preferred_element_type=jnp.float32,
    )
    grad_used = jnp.take(
        token_grads.reshape(tokens_all, col_blocks, BLOCK), down_blocks, axis=1
    ).reshape(tokens_all, DACT * BLOCK)
    product = lax.dot_general(
        masked, grad_used, (((0,), (0,)), ((), ())), preferred_element_type=jnp.float32
    )
    scored = (product * virtual).reshape(UF_DEV, DACT, BLOCK)
    filled = jnp.zeros((UF_DEV, col_blocks, BLOCK), jnp.float32).at[:, down_blocks, :].set(scored)
    return filled.reshape(UF_DEV, VF_DEV)


def solution(mesh):
    placed = (
        P("down", "up"),
        P("up", "down"),
        P(None, "up"),
        P("down"),
        P("up", "down"),
        P("up", "down"),
    )
    return jax.shard_map(
        local, mesh=mesh, in_specs=placed, out_specs=P("up", "down"), check_vma=False
    )
```

profile of v0, /device:TPU:0, one launch (start us, length us, event | category | flops | bytes accessed | tf_op | source)
XLA Modules:
  0.0 144.0 jit_solution(9845222064683501501)
XLA Ops:
  6.5 0.0 copy-start
  6.5 0.0 copy-start.4
  6.5 0.0 all-gather.5.cloned.1.call-start
  6.5 0.7 all-gather.5.cloned.1.call-update
  7.3 0.0 all-gather.3.cloned.1.call-start
  7.3 0.7 compare_select_fusion
  8.0 0.0 copy-done
  8.0 0.0 copy-start.1
  8.0 0.2 copy_bitcast_fusion
  8.2 0.7 gather_fusion.1
  8.9 0.0 copy-done.4
  8.9 0.1 broadcast_bitcast_fusion
  9.0 0.9 bitcast_select_fusion
  9.9 0.0 copy-start.3
  9.9 0.0 copy-start.2
  9.9 0.0 all-gather.3.cloned.1.call-update
  9.9 0.0 copy-done.1
  9.9 16.5 %all_gather.13 = bf16[256,1024]{1,0:T(8,128)(2,1)S(1)} all-gather(bf16[32,1024]{1,0:T(8,128)(2,1)S(1)} %copy-done.1), channel_id=1, replica_groups=mesh['up'=8,'down'=4] {'up'}, dimensions={0}, use_global_device_ids=true | all-gather | bytes 589824 | tf_op jit(solution)/shard_map/all_gather | solution.py:15
  26.4 0.2 copy.32
  26.6 0.3 copy.33
  26.9 0.6 gather_fusion
  27.5 0.1 copy.34
  27.7 0.0 copy-done.3
  27.7 0.1 copy.31
  27.8 0.0 copy-done.2
  27.8 10.0 %all_gather.12 = bf16[256,512]{1,0:T(8,128)(2,1)S(1)} all-gather(bf16[64,512]{1,0:T(8,128)(2,1)S(1)} %copy-done.2), channel_id=1, replica_groups=mesh['up'=8,'down'=4] {'down'}, dimensions={0}, use_global_device_ids=true | all-gather | bytes 327680 | tf_op jit(solution)/shard_map/all_gather | solution.py:14
  37.8 0.1 bitcast_select_fusion.1
  38.0 0.1 mul.14
  38.1 0.3 fusion.1
  38.4 31.6 %all-gather.5.cloned.1.call-done = bf16[512,4608]{1,0:T(8,128)(2,1)} async-done(((bf16[512,1152]{1,0:T(8,128)(2,1)}), bf16[512,4608]{1,0:T(8,128)(2,1)}) %all-gather.5.cloned.1.call-update) | async-done | bytes 4718608 | tf_op jit(solution)/shard_map/all_gather | solution.py:26
  70.1 52.9 %all-gather.3.cloned.1.call-done = bf16[4608,512]{1,0:T(8,128)(2,1)} async-done(((bf16[576,512]{1,0:T(8,128)(2,1)}), bf16[4608,512]{1,0:T(8,128)(2,1)}) %all-gather.3.cloned.1.call-update) | async-done | bytes 4718608 | tf_op jit(solution)/shard_map/all_gather | solution.py:33
  122.9 6.1 %fusion = f32[512,512]{0,1:T(8,128)S(1)} fusion(f32[512,512]{0,1:T(8,128)S(1)} %fusion.1, bf16[4608,512]{1,0:T(8,128)(2,1)} %all-gather.3.cloned.1.call-done, bf16[512,4608]{1,0:T(8,128)(2,1)} %all-gather.5.cloned.1.call-done), kind=kOutput, calls=%fused_computation.4 | convolution fusion | flops 2416181248 | bytes 11534336 | tf_op jit(solution)/shard_map/dot_general | solution.py:31
  129.1 1.3 copy.37
  130.4 0.1 broadcast_in_dim.33
  130.5 1.9 %scatter_fusion = f32[512,8,128]{2,0,1:T(8,128)S(1)} fusion(f32[512,8,128]{2,0,1:T(8,128)S(1)} %broadcast_in_dim.33, s32[4]{0:T(128)S(1)} %compare_select_fusion, f32[4,512,128]{2,1,0:T(8,128)} %bitcast.33), kind=kCustom, calls=%fused_computation.2 | custom fusion | bytes 3145744 | tf_op jit(solution)/shard_map/scatter | solution.py:43
  132.4 1.9 %copy.38 = f32[512,8,128]{0,2,1:T(8,128)} copy(f32[512,8,128]{2,0,1:T(8,128)S(1)} %scatter_fusion) | data formatting | bytes 4194304 | tf_op jit(solution)/shard_map/scatter | solution.py:43
  134.3 2.9 %copy.39 = f32[512,1024]{1,0:T(8,128)} copy(f32[512,1024]{0,1:T(8,128)} %bitcast.32) | data formatting | bytes 4194304 | tf_op jit(solution)/shard_map/reshape | solution.py:44
  (4 shorter events, 0.0 us)
Async XLA Ops:
  6.5 1.4 %copy-start = (bf16[576,1024]{1,0:T(8,128)(2,1)S(1)}, bf16[576,1024]{1,0:T(8,128)(2,1)}, u32[]{:S(2)}) copy-start(bf16[576,1024]{1,0:T(8,128)(2,1)} %param.11) | copy-start | bytes 3538948
  6.5 2.3 %copy-start.4 = (s32[4]{0:T(128)S(1)}, s32[4]{0:T(128)}, u32[]{:S(2)}) copy-start(s32[4]{0:T(128)} %param.9) | copy-start | bytes 52
  6.5 63.5 %all-gather.5.cloned.1.call-start = ((), (), s32[]{:S(2)}) async-start(), calls=%async_computation.1 | async-start | bytes 5898240 | tf_op jit(solution)/shard_map/all_gather | solution.py:26
  7.3 115.7 %all-gather.3.cloned.1.call-start = ((), (), s32[]{:S(2)}) async-start(), calls=%async_computation | async-start | bytes 5308416 | tf_op jit(solution)/shard_map/all_gather | solution.py:33
  8.0 2.0 %copy-start.1 = (bf16[32,1024]{1,0:T(8,128)(2,1)S(1)}, bf16[32,1024]{1,0:T(8,128)(2,1)}, u32[]{:S(2)}) copy-start(bf16[32,1024]{1,0:T(8,128)(2,1)} %param.7) | copy-start | bytes 196612
  9.9 17.8 %copy-start.3 = (s32[8,2]{0,1:T(2,128)S(1)}, s32[8,2]{0,1:T(2,128)}, u32[]{:S(2)}) copy-start(s32[8,2]{0,1:T(2,128)} %param.8) | copy-start | bytes 196
  9.9 17.9 %copy-start.2 = (bf16[64,512]{1,0:T(8,128)(2,1)S(1)}, bf16[64,512]{1,0:T(8,128)(2,1)}, u32[]{:S(2)}) copy-start(bf16[64,512]{1,0:T(8,128)(2,1)} %param.6) | copy-start | bytes 196612
Sparse Core Ops, SparseCore 0:
  9.2 60.8 all-gather.4
  71.7 51.1 all-gather.2
where the time goes:
time: 144 us
  waiting for transfers between devices  85.2 us (59%)
  blocking collectives  26.5 us (18%)
  between operations  13.5 us (9%)
  local copies, waits for them, and re-layouts  10.6 us (7%)
  matrix products  6.41 us (4%)
  other arithmetic  1.76 us (1%)
    all_gather x1, waiting for transfers between devices, local(): lax.all_gather(enc_used, 'up', axis=0, tiled=True)  52.9 us
    all_gather x1, waiting for transfers between devices, local(): dec_whole = lax.all_gather(decoder, 'down', axis=1, tiled=True)  31.6 us
    all_gather x1, blocking collectives, local(): token_grads = lax.all_gather(gradients, 'up', axis=0, tiled=True)  16.5 us
    all_gather x1, blocking collectives, local(): token_deltas = lax.all_gather(deltas, 'down', axis=0, tiled=True)  10 us
    dot_general x1, matrix products, local(): jnp.dot(dec_whole, lax.all_gather(enc_used, 'up', axis=0, tiled=True), pr...  6.1 us
    scatter x2, local copies, waits for them, and re-layouts, local(): jnp.zeros((UF_DEV, col_blocks, BLOCK), jnp.float32).at[:, down_blocks, :]  3.82 us
  transfers between devices with their start and end apart: 2, of which 2 were waited for; matrix products, arithmetic and copies ran while one was open for 3% of the time, Pallas kernels for 0%

commit v1 on v0

--- a/solution.py
+++ b/solution.py
@@ -11,6 +11,11 @@
 
 
 def local(deltas, gradients, up_blocks, down_blocks, decoder, encoder):
+
+    def load_the_vector(xin):
+        y = jnp.concatenate(lax.all_gather(xin, "down"), axis=1)
+        return y
+
     token_deltas = lax.all_gather(deltas, "down", axis=0, tiled=True)
     token_grads = lax.all_gather(gradients, "up", axis=0, tiled=True)
     tokens_all = token_deltas.shape[0]
@@ -23,7 +28,7 @@
         :, None, :, None
     ].astype(token_deltas.dtype)
     masked = masked.reshape(tokens_all, UF_DEV)
-    dec_whole = lax.all_gather(decoder, "down", axis=1, tiled=True)
+    dec_whole = load_the_vector(decoder)
     enc_height = encoder.shape[0]
     enc_used = jnp.take(
         encoder.reshape(enc_height, col_blocks, BLOCK), down_blocks, axis=1

time: 144 us -> 144 us (level)
  waiting for transfers between devices: 85.2 us -> 78.6 us
  local copies, waits for them, and re-layouts: 10.6 us -> 17.2 us
    all_gather x1, waiting for transfers between devices: 52.9 us -> 46.2 us  [local(): lax.all_gather(enc_used, 'up', axis=0, tiled=True)]
    reshape x0 -> x1, local copies, waits for them, and re-layouts: none -> 6.64 us  [load_the_vector(): y = jnp.concatenate(lax.all_gather(xin, 'down'), axis=1)]
  transfers between devices with their start and end apart: 2 -> 2, of which waited for: 2 -> 2; matrix products, arithmetic and copies ran while one was open for 3% -> 8% of each run, Pallas kernels for 0% -> 0%
where the time goes in v1:
time: 144 us
  waiting for transfers between devices  78.6 us (55%)
  blocking collectives  26.5 us (18%)
  local copies, waits for them, and re-layouts  17.2 us (12%)
  between operations  13.5 us (9%)
  matrix products  6.38 us (4%)
  other arithmetic  1.75 us (1%)
    all_gather x1, waiting for transfers between devices, local(): lax.all_gather(enc_used, 'up', axis=0, tiled=True)  46.2 us
    all_gather x1, waiting for transfers between devices, load_the_vector(): y = jnp.concatenate(lax.all_gather(xin, 'down'), axis=1)  31.6 us
    all_gather x1, blocking collectives, local(): token_grads = lax.all_gather(gradients, 'up', axis=0, tiled=True)  16.5 us
    all_gather x1, blocking collectives, local(): token_deltas = lax.all_gather(deltas, 'down', axis=0, tiled=True)  10 us
    reshape x1, local copies, waits for them, and re-layouts, load_the_vector(): y = jnp.concatenate(lax.all_gather(xin, 'down'), axis=1)  6.64 us
    dot_general x1, matrix products, local(): jnp.dot(dec_whole, lax.all_gather(enc_used, 'up', axis=0, tiled=True), pr...  6.07 us
    scatter x2, local copies, waits for them, and re-layouts, local(): jnp.zeros((UF_DEV, col_blocks, BLOCK), jnp.float32).at[:, down_blocks, :]  3.82 us
  transfers between devices with their start and end apart: 2, of which 2 were waited for; matrix products, arithmetic and copies ran while one was open for 8% of the time, Pallas kernels for 0%

profile of v1, /device:TPU:0, one launch (start us, length us, event | category | flops | bytes accessed | tf_op | source)
XLA Modules:
  0.0 144.0 jit_solution(8469344675532432315)
XLA Ops:
  6.5 0.0 copy-start
  6.5 0.0 copy-start.4
  6.5 0.0 all-gather.6.cloned.1.call-start
  6.5 0.7 all-gather.6.cloned.1.call-update
  7.3 0.0 all-gather.4.cloned.1.call-start
  7.3 0.7 compare_select_fusion
  8.0 0.0 copy-done
  8.0 0.0 copy-start.3
  8.0 0.0 copy-start.1
  8.0 0.2 copy_bitcast_fusion
  8.2 0.7 gather_fusion.1
  8.9 0.0 copy-done.4
  8.9 0.1 broadcast_bitcast_fusion
  9.0 0.9 bitcast_select_fusion
  9.9 0.0 copy-start.2
  9.9 0.0 all-gather.4.cloned.1.call-update
  9.9 0.0 copy-done.3
  10.0 0.1 copy.33
  10.1 0.0 copy-done.1
  10.1 16.5 %all_gather.16 = bf16[256,1024]{1,0:T(8,128)(2,1)S(1)} all-gather(bf16[32,1024]{1,0:T(8,128)(2,1)S(1)} %copy-done.1), channel_id=1, replica_groups=mesh['up'=8,'down'=4] {'up'}, dimensions={0}, use_global_device_ids=true | all-gather | bytes 589824 | tf_op jit(solution)/shard_map/all_gather | solution.py:20
  26.6 0.2 copy.34
  26.8 0.3 copy.35
  27.0 0.6 gather_fusion
  27.6 0.1 copy.36
  27.8 0.0 copy-done.2
  27.8 10.0 %all_gather.15 = bf16[256,512]{1,0:T(8,128)(2,1)S(1)} all-gather(bf16[64,512]{1,0:T(8,128)(2,1)S(1)} %copy-done.2), channel_id=1, replica_groups=mesh['up'=8,'down'=4] {'down'}, dimensions={0}, use_global_device_ids=true | all-gather | bytes 327680 | tf_op jit(solution)/shard_map/all_gather | solution.py:19
  37.8 0.1 bitcast_select_fusion.1
  38.0 0.1 mul.14
  38.1 0.3 fusion.1
  38.4 31.6 %all-gather.6.cloned.1.call-done = bf16[2048,1152]{1,0:T(8,128)(2,1)} async-done(((bf16[512,1152]{1,0:T(8,128)(2,1)}), bf16[2048,1152]{1,0:T(8,128)(2,1)}) %all-gather.6.cloned.1.call-update) | async-done | bytes 4718608 | tf_op jit(solution)/shard_map/all_gather | solution.py:16
  70.1 6.6 %copy.39 = bf16[512,4,1152]{0,2,1:T(8,128)(2,1)} copy(bf16[512,4,1152]{2,0,1:T(8,128)(2,1)} %bitcast.39) | data formatting | bytes 9437184 | tf_op jit(solution)/shard_map/reshape | solution.py:16
  76.7 46.2 %all-gather.4.cloned.1.call-done = bf16[4608,512]{1,0:T(8,128)(2,1)} async-done(((bf16[576,512]{1,0:T(8,128)(2,1)}), bf16[4608,512]{1,0:T(8,128)(2,1)}) %all-gather.4.cloned.1.call-update) | async-done | bytes 4718608 | tf_op jit(solution)/shard_map/all_gather | solution.py:38
  122.9 6.1 %fusion = f32[512,512]{0,1:T(8,128)S(1)} fusion(f32[512,512]{0,1:T(8,128)S(1)} %fusion.1, bf16[4608,512]{1,0:T(8,128)(2,1)} %all-gather.4.cloned.1.call-done, bf16[512,4608]{0,1:T(8,128)(2,1)} %bitcast.37), kind=kOutput, calls=%fused_computation.4 | convolution fusion | flops 2416181248 | bytes 11534336 | tf_op jit(solution)/shard_map/dot_general | solution.py:36
  129.0 1.3 copy.40
  130.3 0.1 broadcast_in_dim.33
  130.5 1.9 %scatter_fusion = f32[512,8,128]{2,0,1:T(8,128)S(1)} fusion(f32[512,8,128]{2,0,1:T(8,128)S(1)} %broadcast_in_dim.33, s32[4]{0:T(128)S(1)} %compare_select_fusion, f32[4,512,128]{2,1,0:T(8,128)} %bitcast.41), kind=kCustom, calls=%fused_computation.2 | custom fusion | bytes 3145744 | tf_op jit(solution)/shard_map/scatter | solution.py:48
  132.4 1.9 %copy.41 = f32[512,8,128]{0,2,1:T(8,128)} copy(f32[512,8,128]{2,0,1:T(8,128)S(1)} %scatter_fusion) | data formatting | bytes 4194304 | tf_op jit(solution)/shard_map/scatter | solution.py:48
  134.3 2.9 %copy.42 = f32[512,1024]{1,0:T(8,128)} copy(f32[512,1024]{0,1:T(8,128)} %bitcast.38) | data formatting | bytes 4194304 | tf_op jit(solution)/shard_map/reshape | solution.py:49
  (4 shorter events, 0.0 us)
Async XLA Ops:
  6.5 1.4 %copy-start = (bf16[576,1024]{1,0:T(8,128)(2,1)S(1)}, bf16[576,1024]{1,0:T(8,128)(2,1)}, u32[]{:S(2)}) copy-start(bf16[576,1024]{1,0:T(8,128)(2,1)} %param.11) | copy-start | bytes 3538948
  6.5 2.4 %copy-start.4 = (s32[4]{0:T(128)S(1)}, s32[4]{0:T(128)}, u32[]{:S(2)}) copy-start(s32[4]{0:T(128)} %param.9) | copy-start | bytes 52
  6.5 63.5 %all-gather.6.cloned.1.call-start = ((), (), s32[]{:S(2)}) async-start(), calls=%async_computation.1 | async-start | bytes 5898240 | tf_op jit(solution)/shard_map/all_gather | solution.py:16
  7.3 115.7 %all-gather.4.cloned.1.call-start = ((), (), s32[]{:S(2)}) async-start(), calls=%async_computation | async-start | bytes 5308416 | tf_op jit(solution)/shard_map/all_gather | solution.py:38
  8.0 2.0 %copy-start.3 = (s32[8,2]{0,1:T(2,128)S(1)}, s32[8,2]{0,1:T(2,128)}, u32[]{:S(2)}) copy-start(s32[8,2]{0,1:T(2,128)} %param.8) | copy-start | bytes 196
  8.0 2.1 %copy-start.1 = (bf16[32,1024]{1,0:T(8,128)(2,1)S(1)}, bf16[32,1024]{1,0:T(8,128)(2,1)}, u32[]{:S(2)}) copy-start(bf16[32,1024]{1,0:T(8,128)(2,1)} %param.7) | copy-start | bytes 196612
  9.9 17.9 %copy-start.2 = (bf16[64,512]{1,0:T(8,128)(2,1)S(1)}, bf16[64,512]{1,0:T(8,128)(2,1)}, u32[]{:S(2)}) copy-start(bf16[64,512]{1,0:T(8,128)(2,1)} %param.6) | copy-start | bytes 196612
Sparse Core Ops, SparseCore 0:
  9.2 60.8 all-gather.5
  71.7 51.1 all-gather.3
